TPU v7x, 16 devices: a 4x2x1 block of a 4x4x8 slice. The times are simulated.
16 devices in a mesh: rep: 4 (over y, z, core), dp: 4 (over x).
Axes of the slice: x: 4, y: 2, z: 1, core: 2. Of those that a mesh axis runs over, the one named last changes fastest.
The devices are a block of a 4x4x8 slice.
Arguments:
- a: bfloat16 [16, 4, 8192, 512], P(('rep', 'dp')), parts along dimension 0
- g: bfloat16 [16, 4, 8192, 1408], P(('rep', 'dp')), parts along dimension 0
Outputs:
- output: bfloat16 [16, 512, 1408], P('rep'), parts along dimension 0
There are 4 independent parts. A program takes and returns all parts, laid end to end along the dimension named above; each array names one.
All inputs are finite; a program needn't handle non-finite values.
Results may differ from a plain program's by a relative error of at most 0.012.
Values are sent between devices in bfloat16 or wider.
A program may use at most 768 MiB of HBM per device.

v0:
```python
import jax
import jax.numpy as jnp


def solution(mesh):
    groups = mesh.shape["rep"]

    def step(a, g):
        a, g = (t.reshape(groups, -1, *t.shape[1:]) for t in (a, g))
        sums = jnp.einsum("rsntd,rsntf->rndf", a, g, preferred_element_type=jnp.float32)
        return sums.astype(jnp.bfloat16).reshape(-1, *sums.shape[2:])

    return step
```

profile of v0, /device:TPU:112, one launch (start us, length us, event | category | flops | bytes accessed | tf_op | source)
XLA Modules:
  0.0 265.6 jit_solution(12647451621746465220)
XLA Ops:
  0.0 63.0 %fusion.3 = f32[1,4,512,1408]{3,2,1,0:T(8,128)} fusion(bf16[1,4,8192,1408]{3,2,1,0:T(8,128)(2,1)} %param.1, bf16[1,4,8192,512]{3,2,1,0:T(8,128)(2,1)} %param), kind=kOutput, calls=%fused_computation.3 | convolution fusion | flops 47244640256 | bytes 137363456 | tf_op jit(solution)/rsntd,rsntf->rndf/dot_general | solution.py:10
  63.0 202.7 %all-reduce.2 = bf16[1,4,512,1408]{3,2,1,0:T(8,128)(2,1)} all-reduce(f32[1,4,512,1408]{3,2,1,0:T(8,128)} %fusion.3), channel_id=1, replica_groups=[4,4]<=[16], use_global_device_ids=true, to_apply=%add.clone | all-reduce | flops 2883584 | bytes 17301504 | tf_op jit(solution)/rsntd,rsntf->rndf/dot_general | solution.py:10
where the time goes:
time: 266 us
  blocking collectives  203 us (76%)
  matrix products  63 us (24%)
    dot_general x1, blocking collectives, step(): jnp.einsum('rsntd,rsntf->rndf', a, g, preferred_element_type=jnp.float32)  203 us
    dot_general x1, matrix products, step(): jnp.einsum('rsntd,rsntf->rndf', a, g, preferred_element_type=jnp.float32)  63 us

commit v1 on v0

v1 whole, which is shorter than its diff:
```python
import functools

import jax
import jax.numpy as jnp
from jax import lax
from jax.experimental import pallas as pl
from jax.experimental.pallas import tpu as pltpu

WIDE = 256
SLOTS = 4
PIECES = 4
RIGHT, LEFT = 0, 1


def kernel(axis, group, a_hbm, g_hbm, out, a_buf, g_buf, first, landed, a_sem, a0_sem, g_sem, g0_sem, send_sem, recv_sem):
    tokens, rows = a_hbm.shape[1:]
    columns = g_hbm.shape[2]
    half = rows // 2
    narrow = columns % WIDE or WIDE
    chunks = 1 + (columns - narrow) // WIDE
    me = lax.axis_index(axis)
    ring = [lax.rem(me + k, group) for k in range(group)]
    peer = (ring[1], ring[group - 1])

    def width(j):
        return narrow if isinstance(j, int) and j == 0 else WIDE

    def start_column(j):
        if isinstance(j, int):
            return 0 if j == 0 else narrow + (j - 1) * WIDE
        return pl.multiple_of(narrow + (j - 1) * WIDE, 128)

    def cols(j):
        return pl.ds(start_column(j), width(j))

    def half_rows(side):
        return pl.ds(side * half, half)

    def matrix(phase, side):
        return ring[(group - 1 - phase) % group] if side == RIGHT else ring[(phase + 1) % group]

    def g_load(m, j, slot):
        step = tokens // PIECES
        for p in range(PIECES):
            rows_p = pl.ds(p * step, step)
            pltpu.make_async_copy(
                g_hbm.at[m, rows_p, cols(j)], g_buf.at[slot, rows_p, pl.ds(0, width(j))], g_sem.at[slot]
            ).start()

    def g_wait(j, slot):
        pltpu.make_async_copy(
            g_hbm.at[0, :, cols(j)], g_buf.at[slot, :, pl.ds(0, width(j))], g_sem.at[slot]
        ).wait()

    def a_load(phase, side):
        pltpu.make_async_copy(
            a_hbm.at[matrix(phase, side), :, half_rows(side)],
            a_buf.at[phase % 2, :, half_rows(side)],
            a_sem.at[phase % 2, side],
        ).start()

    def a_wait(phase, side):
        pltpu.make_async_copy(
            a_hbm.at[0, :, half_rows(side)], a_buf.at[phase % 2, :, half_rows(side)], a_sem.at[phase % 2, side]
        ).wait()

    def piece_copies(side, p):
        step = tokens // PIECES
        rows_p = pl.ds(p * step, step)
        m = matrix(0, side)
        return (
            pltpu.make_async_copy(
                a_hbm.at[m, rows_p, half_rows(side)], a_buf.at[0, rows_p, half_rows(side)], a0_sem.at[side, p]
            ),
            pltpu.make_async_copy(
                g_hbm.at[m, rows_p, cols(0)], g_buf.at[side, rows_p, pl.ds(0, narrow)], g0_sem.at[side, p]
            ),
        )

    def hop(side, n, j):
        if n < group - 1:
            src = (first if n == 0 else landed.at[n - 1]).at[side, j, :, pl.ds(0, width(j))]
            dst = landed.at[n, side, j, :, pl.ds(0, width(j))]
        else:
            k = n - (group - 1)
            m = ring[(group - k) % group] if side == RIGHT else ring[k]
            src = dst = out.at[m, half_rows(side), cols(j)]
        return pltpu.make_async_remote_copy(
            src_ref=src,
            dst_ref=dst,
            send_sem=send_sem.at[side, n, j],
            recv_sem=recv_sem.at[side, n, j],
            device_id={axis: peer[side]},
            device_id_type=pl.DeviceIdType.MESH,
        )

    def arrived(side, n, j):
        if n < group - 1:
            return hop(side, n, j)
        k = n - (group - 1) + 1
        m = ring[(group - k) % group] if side == RIGHT else ring[k % group]
        ref = out.at[m, half_rows(side), cols(j)]
        return pltpu.make_async_remote_copy(
            src_ref=ref,
            dst_ref=ref,
            send_sem=send_sem.at[side, n, j],
            recv_sem=recv_sem.at[side, n, j],
            device_id={axis: peer[side]},
            device_id_type=pl.DeviceIdType.MESH,
        )

    def product(a, g):
        return lax.dot_general(a, g, (((0,), (0,)), ((), ())), preferred_element_type=jnp.float32)

    def pass_on(phase, side, j, term):
        w = width(j)
        if phase == 0:
            first[side, j, :, pl.ds(0, w)] = term.astype(first.dtype)
        else:
            arrived(side, phase - 1, j).wait_recv()
            total = (landed[phase - 1, side, j, :, pl.ds(0, w)].astype(jnp.float32) + term).astype(first.dtype)
            if phase < group - 1:
                landed[phase - 1, side, j, :, pl.ds(0, w)] = total
            else:
                out[me, half_rows(side), cols(j)] = total
        hop(side, phase, j).start()

    split = [True, False, True, False]
    base = [0, 2 * chunks, 3 * chunks, 5 * chunks]
    total_blocks = 6 * chunks

    def slot_of(phase, j, side):
        return (base[phase] + (2 * j + side if split[phase] else j)) % SLOTS

    def refill(phase, j, side):
        def fetch(q, jj, ss):
            g_load(matrix(q, ss), jj, slot_of(q, jj, ss))

        def later(q, flat):
            if split[q]:
                raise AssertionError
            fetch(q, flat, RIGHT)

        if split[phase]:
            if isinstance(j, int):
                flat = 2 * j + side + SLOTS
                if flat < 2 * chunks:
                    fetch(phase, flat // 2, flat % 2)
                else:
                    fetch(phase + 1, flat - 2 * chunks, RIGHT)
                return
            near = chunks - SLOTS // 2

            @pl.when(j < near)
            def _():
                fetch(phase, j + SLOTS // 2, side)

            if side == RIGHT:
                @pl.when(j == near)
                def _():
                    fetch(phase + 1, 0, RIGHT)

            @pl.when(j > near if side == RIGHT else j >= near)
            def _():
                fetch(phase + 1, 2 * (j - near) + side, RIGHT)
        else:
            near = chunks - SLOTS
            if isinstance(j, int):
                assert j < near
                fetch(phase, j + SLOTS, RIGHT)
                return

            @pl.when(j < near)
            def _():
                fetch(phase, j + SLOTS, RIGHT)

            if phase + 1 < len(split):
                for k in range(SLOTS):
                    @pl.when(j == near + k)
                    def _(k=k):
                        fetch(phase + 1, k // 2, k % 2)

    for side in (RIGHT, LEFT):
        for p in range(PIECES):
            for copy in piece_copies(side, p):
                copy.start()
    for side in (RIGHT, LEFT):
        g_load(matrix(0, side), 1, slot_of(0, 1, side))

    barrier = pltpu.get_barrier_semaphore()
    for side in (RIGHT, LEFT):
        pl.semaphore_signal(barrier, inc=1, device_id={axis: peer[side]}, device_id_type=pl.DeviceIdType.MESH)

    step = tokens // PIECES
    for side in (RIGHT, LEFT):
        term = None
        for p in range(PIECES):
            for copy in piece_copies(side, p):
                copy.wait()
            rows_p = pl.ds(p * step, step)
            part = product(a_buf[0, rows_p, half_rows(side)], g_buf[side, rows_p, pl.ds(0, narrow)])
            term = part if term is None else term + part
        if side == RIGHT:
            pl.semaphore_wait(barrier, 2)
        pass_on(0, side, 0, term)
        refill(0, 0, side)

    def block(phase, j):
        w = width(j)
        if split[phase]:
            for side in (RIGHT, LEFT):
                slot = slot_of(phase, j, side)
                g_wait(j, slot)
                term = product(a_buf[phase % 2, :, half_rows(side)], g_buf[slot, :, pl.ds(0, w)])
                pass_on(phase, side, j, term)
                refill(phase, j, side)
        else:
            slot = slot_of(phase, j, RIGHT)
            g_wait(j, slot)
            terms = product(a_buf[phase % 2], g_buf[slot, :, pl.ds(0, w)])
            for side in (RIGHT, LEFT):
                pass_on(phase, side, j, terms[side * half:(side + 1) * half])
            refill(phase, j, RIGHT)

    for phase in range(len(split)):
        if phase + 1 < len(split):
            for side in (RIGHT, LEFT):
                a_load(phase + 1, side)
        if phase > 0:
            for side in (RIGHT, LEFT):
                a_wait(phase, side)
            block(phase, 0)
        lax.fori_loop(1, chunks, lambda j, _, phase=phase: (block(phase, j), 0)[1], 0)

    last = 2 * (group - 1)
    for n in range(group - 1, last - 1):
        for j in range(chunks):
            for side in (RIGHT, LEFT):
                arrived(side, n, j).wait_recv()
                hop(side, n + 1, j).start()
    for j in range(chunks):
        for side in (RIGHT, LEFT):
            arrived(side, last - 1, j).wait_recv()
    for n in range(last):
        for j in range(chunks):
            for side in (RIGHT, LEFT):
                hop(side, n, j).wait_send()


def solution(mesh):
    axis = "dp"
    group = mesh.shape[axis]

    def sums(a, g):
        a, g = a.reshape(a.shape[1:]), g.reshape(g.shape[1:])
        matrices, tokens, rows = a.shape
        columns = g.shape[2]
        narrow = columns % WIDE or WIDE
        chunks = 1 + (columns - narrow) // WIDE
        half = rows // 2
        hops = 2 * (group - 1)
        return pl.pallas_call(
            functools.partial(kernel, axis, group),
            out_shape=pltpu.VMEM((matrices, rows, columns), a.dtype),
            in_specs=[pl.BlockSpec(memory_space=pltpu.HBM)] * 2,
            out_specs=pl.BlockSpec(memory_space=pltpu.VMEM),
            scratch_shapes=[
                pltpu.VMEM((2, tokens, rows), a.dtype),
                pltpu.VMEM((SLOTS, tokens, WIDE), a.dtype),
                pltpu.VMEM((2, chunks, half, WIDE), a.dtype),
                pltpu.VMEM((group - 1, 2, chunks, half, WIDE), a.dtype),
                pltpu.SemaphoreType.DMA((2, 2)),
                pltpu.SemaphoreType.DMA((2, PIECES)),
                pltpu.SemaphoreType.DMA((SLOTS,)),
                pltpu.SemaphoreType.DMA((2, PIECES)),
                pltpu.SemaphoreType.DMA((2, hops, chunks)),
                pltpu.SemaphoreType.DMA((2, hops, chunks)),
            ],
            compiler_params=pltpu.CompilerParams(
                collective_id=0, has_side_effects=True, vmem_limit_bytes=52 * 2**20
            ),
            cost_estimate=pl.CostEstimate(
                flops=2 * matrices * tokens * rows * columns,
                bytes_accessed=2 * matrices * tokens * (rows + columns),
                transcendentals=0,
            ),
            name="sums",
        )(a, g)

    spec = jax.P(("rep", axis))
    return jax.shard_map(sums, mesh=mesh, in_specs=(spec, spec), out_specs=jax.P("rep"), check_vma=False)
```

time: 266 us -> 132 us (0.50)
  blocking collectives: 203 us -> 0 us
  Pallas kernels: 0 us -> 129 us
  matrix products: 63 us -> 0 us
    dot_general x1 -> x0, blocking collectives: 203 us -> none  [step(): jnp.einsum('rsntd,rsntf->rndf', a, g, preferred_element_type=jnp.float32)]
    pallas_call x0 -> x1, Pallas kernels: none -> 129 us  [sums(): pl.pallas_call(functools.partial(kernel, axis, group), out_shape=pltpu.VM...]
    dot_general x1 -> x0, matrix products: 63 us -> none  [step(): jnp.einsum('rsntd,rsntf->rndf', a, g, preferred_element_type=jnp.float32)]
where the time goes in v1:
time: 132 us
  Pallas kernels  129 us (98%)
  local copies, waits for them, and re-layouts  2.53 us (2%)
    pallas_call x1, Pallas kernels, sums(): pl.pallas_call(functools.partial(kernel, axis, group), out_shape=pltpu.VM...  129 us

profile of v1, /device:TPU:112, one launch (start us, length us, event | category | flops | bytes accessed | tf_op | source)
XLA Modules:
  0.0 131.6 jit_solution(16865611175427630035)
XLA Ops:
  0.0 129.0 %sums.1 = bf16[4,512,1408]{2,1,0:T(8,128)(2,1)S(1)} custom-call(bf16[4,8192,512]{2,1,0:T(8,128)(2,1)} %bitcast.2, bf16[4,8192,1408]{2,1,0:T(8,128)(2,1)} %bitcast.1.g_hbm), custom_call_target="tpu_custom_call" | custom-call | flops 47244640256 | bytes 125829120 | tf_op jit(solution)/shard_map/sums/pallas_call | solution.py:262
  129.1 2.5 %copy.4 = bf16[4,512,1408]{2,1,0:T(8,128)(2,1)} copy(bf16[4,512,1408]{2,1,0:T(8,128)(2,1)S(1)} %sums.1) | data formatting | bytes 11534336

commit v2 on v0

v2 whole, which is shorter than its diff:
```python
import functools

import jax
import jax.numpy as jnp
from jax import lax
from jax.experimental import pallas as pl
from jax.experimental.pallas import tpu as pltpu

TILE = 128
WIDE = 2 * TILE
SLOTS = 4
PIECES = 4
RIGHT, LEFT = 0, 1
GROUP = 4
HOPS = 2 * (GROUP - 1)


def kernel(axis, a_hbm, g_hbm, out, a_buf, g_buf, terms, first, landed, a_sem, a0_sem, g_sem, g0_sem, send_sem, recv_sem):
    matrices, tokens, rows = a_hbm.shape
    columns = g_hbm.shape[2]
    half = rows // 2
    pairs = columns // WIDE
    wide_units = matrices * pairs // 2
    units = wide_units + 1
    blocks = matrices * (pairs + 1)
    cycle = 2 * (pairs + 1)
    me = lax.axis_index(axis)
    ring = [lax.rem(me + k, GROUP) for k in range(GROUP)]
    peer = (ring[1], ring[GROUP - 1])

    def half_rows(side):
        return pl.ds(side * half, half)

    def block_place(i):
        group, q = i // cycle, i % cycle
        narrow = q // (pairs + 1) - q // (pairs + 2) + q // (cycle - 1)
        r = q - q // (pairs + 2)
        unit, second = group * pairs + r // 2, r % 2
        pair = 2 * unit + second * (me % 2) + (1 - second) * (1 - me % 2)
        narrow_m = 2 * group + q // (cycle - 1)
        m = narrow * narrow_m + (1 - narrow) * (pair // pairs)
        column = narrow * (columns - WIDE) + (1 - narrow) * (pair % pairs) * WIDE
        kept = narrow * (2 * wide_units + narrow_m) + (1 - narrow) * (2 * unit + second)
        return m, pl.multiple_of(column, TILE), kept

    def g_load(i):
        m, column, _ = block_place(i)
        slot = i % SLOTS
        step = tokens // PIECES
        for p in range(PIECES):
            rows_p = pl.ds(p * step, step)
            pltpu.make_async_copy(
                g_hbm.at[m, rows_p, pl.ds(column, WIDE)], g_buf.at[slot, rows_p], g_sem.at[slot]
            ).start()

    def g_wait(i):
        slot = i % SLOTS
        pltpu.make_async_copy(g_hbm.at[0, :, pl.ds(0, WIDE)], g_buf.at[slot], g_sem.at[slot]).wait()

    def a_load(m):
        return pltpu.make_async_copy(a_hbm.at[m], a_buf.at[m % 2], a_sem.at[m % 2])

    def piece_copies(p):
        step = tokens // PIECES
        rows_p = pl.ds(p * step, step)
        m, column, _ = block_place(0)
        return (
            pltpu.make_async_copy(a_hbm.at[m, rows_p], a_buf.at[0, rows_p], a0_sem.at[p]),
            pltpu.make_async_copy(g_hbm.at[m, rows_p, pl.ds(column, WIDE)], g_buf.at[0, rows_p], g0_sem.at[p]),
        )

    def tile_place(u, owner):
        if isinstance(u, int) and u == wide_units:
            return owner, columns - TILE
        pair = 2 * u + owner % 2
        return pair // pairs, pl.multiple_of((pair % pairs) * WIDE + (owner // 2) * TILE, TILE)

    def term_of(u, k, side):
        owner = ring[k]
        if isinstance(u, int) and u == wide_units:
            return terms[2 * wide_units + owner, half_rows(side), pl.ds(TILE, TILE)]
        return terms[2 * u + 1 - k % 2, half_rows(side), pl.ds(pl.multiple_of((owner // 2) * TILE, TILE), TILE)]

    def out_tile(u, k, side):
        m, column = tile_place(u, ring[k])
        return out.at[m, half_rows(side), pl.ds(column, TILE)]

    def whose(side, n):
        k = (GROUP - 1 - n) % GROUP
        return k if side == RIGHT else (GROUP - k) % GROUP

    def remote(side, n, u, src, dst):
        return pltpu.make_async_remote_copy(
            src_ref=src,
            dst_ref=dst,
            send_sem=send_sem.at[side, n, u],
            recv_sem=recv_sem.at[side, n, u],
            device_id={axis: peer[side]},
            device_id_type=pl.DeviceIdType.MESH,
        )

    def hop(side, n, u):
        if n < GROUP - 1:
            return remote(side, n, u, first.at[side, u] if n == 0 else landed.at[n - 1, side, u], landed.at[n, side, u])
        tile = out_tile(u, whose(side, n), side)
        return remote(side, n, u, tile, tile)

    def arrival(side, n, u):
        if n < GROUP - 1:
            return hop(side, n, u)
        tile = out_tile(u, whose(side, n + 1), side)
        return remote(side, n, u, tile, tile)

    def send(n, u):
        for side in (RIGHT, LEFT):
            k = whose(side, n)
            if n == 0:
                first[side, u] = term_of(u, k, side).astype(first.dtype)
            else:
                arrival(side, n - 1, u).wait_recv()
                if n < GROUP:
                    total = (landed[n - 1, side, u].astype(jnp.float32) + term_of(u, k, side)).astype(first.dtype)
                    if n < GROUP - 1:
                        landed[n - 1, side, u] = total
                    else:
                        m, column = tile_place(u, me)
                        out[m, half_rows(side), pl.ds(column, TILE)] = total
            hop(side, n, u).start()

    def product(a, g):
        return lax.dot_general(a, g, (((0,), (0,)), ((), ())), preferred_element_type=jnp.float32)

    for p in range(PIECES):
        for copy in piece_copies(p):
            copy.start()
    for i in range(1, SLOTS):
        g_load(i)
    a_load(1).start()

    barrier = pltpu.get_barrier_semaphore()
    for side in (RIGHT, LEFT):
        pl.semaphore_signal(barrier, inc=1, device_id={axis: peer[side]}, device_id_type=pl.DeviceIdType.MESH)

    step = tokens // PIECES
    term = None
    for p in range(PIECES):
        for copy in piece_copies(p):
            copy.wait()
        part = product(a_buf[0, pl.ds(p * step, step)], g_buf[0, pl.ds(p * step, step)])
        term = part if term is None else term + part
    terms[0] = term
    g_load(SLOTS)
    pl.semaphore_wait(barrier, 2)
    send(0, 0)

    def body(i, _):
        m, _, kept = block_place(i)
        group, q = i // cycle, i % cycle
        @pl.when(i == pairs - 1)
        def _():
            a_load(1).wait()

        @pl.when(i == cycle)
        def _():
            a_load(2).wait()

        @pl.when(i == cycle + pairs - 1)
        def _():
            a_load(3).wait()

        g_wait(i)
        terms[kept] = product(a_buf[m % 2], g_buf[i % SLOTS])

        @pl.when(i + SLOTS < blocks)
        def _():
            g_load(i + SLOTS)

        @pl.when(i == pairs + 1)
        def _():
            a_load(2).start()

        @pl.when(i == cycle - 1)
        def _():
            a_load(3).start()

        narrow = q // (pairs + 1) - q // (pairs + 2) + q // (cycle - 1)
        r = q - q // (pairs + 2)
        u, second = group * pairs + r // 2, r % 2
        kind = 2 * narrow + second

        @pl.when(kind == 0)
        def _():
            send(0, u)

            @pl.when(u >= 1)
            def _():
                send(1, u - 1)

        @pl.when((kind == 1) & (u >= 2))
        def _():
            send(2, u - 2)

            @pl.when(u >= 3)
            def _():
                send(3, u - 3)

        return 0

    lax.fori_loop(1, blocks, body, 0)

    last = wide_units
    late = [(0, last), (1, last - 1), (2, last - 2), (3, last - 3), None,
            (1, last), (2, last - 1), (3, last - 2), None,
            (2, last), (3, last - 1), None, (3, last), None]
    fill = [(4, u) for u in range(units - 3)] + [(5, u) for u in range(3)]
    for item in late:
        if item is not None:
            send(*item)
        else:
            for _ in range(3):
                if fill:
                    send(*fill.pop(0))
    for item in fill:
        send(*item)
    for u in range(units - 3, units):
        send(4, u)
    for u in range(3, units):
        send(5, u)
    for u in range(units):
        for side in (RIGHT, LEFT):
            arrival(side, HOPS - 1, u).wait_recv()
    for n in range(HOPS):
        for u in range(units):
            for side in (RIGHT, LEFT):
                hop(side, n, u).wait_send()


def solution(mesh):
    axis = "dp"

    def sums(a, g):
        a, g = a.reshape(a.shape[1:]), g.reshape(g.shape[1:])
        matrices, tokens, rows = a.shape
        columns = g.shape[2]
        pairs = columns // WIDE
        units = matrices * pairs // 2 + 1
        half = rows // 2
        assert mesh.shape[axis] == GROUP == matrices and columns % WIDE == TILE
        return pl.pallas_call(
            functools.partial(kernel, axis),
            out_shape=pltpu.VMEM((matrices, rows, columns), a.dtype),
            in_specs=[pl.BlockSpec(memory_space=pltpu.HBM)] * 2,
            out_specs=pl.BlockSpec(memory_space=pltpu.VMEM),
            scratch_shapes=[
                pltpu.VMEM((2, tokens, rows), a.dtype),
                pltpu.VMEM((SLOTS, tokens, WIDE), a.dtype),
                pltpu.VMEM((matrices * (pairs + 1), rows, WIDE), jnp.float32),
                pltpu.VMEM((2, units, half, TILE), a.dtype),
                pltpu.VMEM((GROUP - 1, 2, units, half, TILE), a.dtype),
                pltpu.SemaphoreType.DMA((2,)),
                pltpu.SemaphoreType.DMA((PIECES,)),
                pltpu.SemaphoreType.DMA((SLOTS,)),
                pltpu.SemaphoreType.DMA((PIECES,)),
                pltpu.SemaphoreType.DMA((2, HOPS, units)),
                pltpu.SemaphoreType.DMA((2, HOPS, units)),
            ],
            compiler_params=pltpu.CompilerParams(
                collective_id=0, has_side_effects=True, vmem_limit_bytes=57 * 2**20
            ),
            cost_estimate=pl.CostEstimate(
                flops=2 * matrices * tokens * rows * columns,
                bytes_accessed=2 * matrices * tokens * (rows + columns),
                transcendentals=0,
            ),
            name="sums",
        )(a, g)

    spec = jax.P(("rep", axis))
    return jax.shard_map(sums, mesh=mesh, in_specs=(spec, spec), out_specs=jax.P("rep"), check_vma=False)
```

time: 266 us -> 126 us (0.47)
  blocking collectives: 203 us -> 0 us
  Pallas kernels: 0 us -> 123 us
  matrix products: 63 us -> 0 us
    dot_general x1 -> x0, blocking collectives: 203 us -> none  [step(): jnp.einsum('rsntd,rsntf->rndf', a, g, preferred_element_type=jnp.float32)]
    pallas_call x0 -> x1, Pallas kernels: none -> 123 us  [sums(): pl.pallas_call(functools.partial(kernel, axis), out_shape=pltpu.VMEM((mat...]
    dot_general x1 -> x0, matrix products: 63 us -> none  [step(): jnp.einsum('rsntd,rsntf->rndf', a, g, preferred_element_type=jnp.float32)]
where the time goes in v2:
time: 126 us
  Pallas kernels  123 us (98%)
  local copies, waits for them, and re-layouts  2.53 us (2%)
    pallas_call x1, Pallas kernels, sums(): pl.pallas_call(functools.partial(kernel, axis), out_shape=pltpu.VMEM((mat...  123 us
    unnamed x1, local copies, waits for them, and re-layouts  2.53 us

profile of v2, /device:TPU:112, one launch (start us, length us, event | category | flops | bytes accessed | tf_op | source)
XLA Modules:
  0.0 125.8 jit_solution(9827062127439381761)
XLA Ops:
  0.0 123.3 %sums.1 = bf16[4,512,1408]{2,1,0:T(8,128)(2,1)S(1)} custom-call(bf16[4,8192,512]{2,1,0:T(8,128)(2,1)} %bitcast.2, bf16[4,8192,1408]{2,1,0:T(8,128)(2,1)} %bitcast.1.g_hbm), custom_call_target="tpu_custom_call" | custom-call | flops 47244640256 | bytes 125829120 | tf_op jit(solution)/shard_map/sums/pallas_call | solution.py:249
  123.3 2.5 %copy.4 = bf16[4,512,1408]{2,1,0:T(8,128)(2,1)} copy(bf16[4,512,1408]{2,1,0:T(8,128)(2,1)S(1)} %sums.1) | data formatting | bytes 11534336

commit v3 on v2

--- a/solution.py
+++ b/solution.py
@@ -13,6 +13,37 @@
 RIGHT, LEFT = 0, 1
 GROUP = 4
 HOPS = 2 * (GROUP - 1)
+SENDS = (
+    ((0, 0),),
+    ((0, 1),),
+    ((1, 0),),
+    ((1, 1),),
+    ((0, 2), (2, 0)),
+    ((2, 1),),
+    ((1, 2), (3, 0)),
+    ((0, 3), (3, 1)),
+    ((2, 2), (4, 0)),
+    ((0, 4), (1, 3), (4, 1)),
+    ((3, 2), (5, 0)),
+    ((1, 4), (2, 3)),
+    ((0, 5), (4, 2), (5, 1)),
+    ((0, 6), (2, 4)),
+    ((1, 5), (3, 3)),
+    ((1, 6), (5, 2)),
+    ((0, 7), (2, 5), (3, 4)),
+    ((2, 6), (4, 3)),
+    ((1, 7), (3, 5)),
+    ((0, 8), (3, 6)),
+    ((2, 7), (4, 4)),
+    ((0, 9), (1, 8), (4, 5)),
+    ((3, 7), (4, 6)),
+    ((0, 10), (1, 9)),
+)
+LATE = (
+    (2, 8), (1, 10), (2, 9), (3, 8), (2, 10), (3, 9), (4, 7), (3, 10),
+    (4, 8), (4, 9), (4, 10), (5, 3), (5, 4), (5, 5), (5, 6), (5, 7),
+    (5, 8), (5, 9), (5, 10),
+)
 
 
 def kernel(axis, a_hbm, g_hbm, out, a_buf, g_buf, terms, first, landed, a_sem, a0_sem, g_sem, g0_sem, send_sem, recv_sem):
@@ -35,6 +66,8 @@
         group, q = i // cycle, i % cycle
         narrow = q // (pairs + 1) - q // (pairs + 2) + q // (cycle - 1)
         r = q - q // (pairs + 2)
+        swap = (r + cycle - 1) // cycle - (r + cycle - 3) // cycle
+        r = swap * (3 - r) + (1 - swap) * r
         unit, second = group * pairs + r // 2, r % 2
         pair = 2 * unit + second * (me % 2) + (1 - second) * (1 - me % 2)
         narrow_m = 2 * group + q // (cycle - 1)
@@ -155,7 +188,6 @@
 
     def body(i, _):
         m, _, kept = block_place(i)
-        group, q = i // cycle, i % cycle
         @pl.when(i == pairs - 1)
         def _():
             a_load(1).wait()
@@ -183,49 +215,19 @@
         def _():
             a_load(3).start()
 
-        narrow = q // (pairs + 1) - q // (pairs + 2) + q // (cycle - 1)
-        r = q - q // (pairs + 2)
-        u, second = group * pairs + r // 2, r % 2
-        kind = 2 * narrow + second
-
-        @pl.when(kind == 0)
-        def _():
-            send(0, u)
-
-            @pl.when(u >= 1)
-            def _():
-                send(1, u - 1)
-
-        @pl.when((kind == 1) & (u >= 2))
-        def _():
-            send(2, u - 2)
-
-            @pl.when(u >= 3)
-            def _():
-                send(3, u - 3)
+        for k in range(1, blocks):
+            if SENDS[k]:
+                @pl.when(i == k)
+                def _(k=k):
+                    for n, u in SENDS[k]:
+                        send(n, u)
 
         return 0
 
     lax.fori_loop(1, blocks, body, 0)
 
-    last = wide_units
-    late = [(0, last), (1, last - 1), (2, last - 2), (3, last - 3), None,
-            (1, last), (2, last - 1), (3, last - 2), None,
-            (2, last), (3, last - 1), None, (3, last), None]
-    fill = [(4, u) for u in range(units - 3)] + [(5, u) for u in range(3)]
-    for item in late:
-        if item is not None:
-            send(*item)
-        else:
-            for _ in range(3):
-                if fill:
-                    send(*fill.pop(0))
-    for item in fill:
-        send(*item)
-    for u in range(units - 3, units):
-        send(4, u)
-    for u in range(3, units):
-        send(5, u)
+    for n, u in LATE:
+        send(n, u)
     for u in range(units):
         for side in (RIGHT, LEFT):
             arrival(side, HOPS - 1, u).wait_recv()

time: 126 us -> 120 us (0.952)
  Pallas kernels: 123 us -> 117 us
    pallas_call x1, Pallas kernels: 123 us -> 117 us  [sums(): pl.pallas_call(functools.partial(kernel, axis), out_shape=pltpu.VMEM((mat...]
where the time goes in v3:
time: 120 us
  Pallas kernels  117 us (98%)
  local copies, waits for them, and re-layouts  2.53 us (2%)
    pallas_call x1, Pallas kernels, sums(): pl.pallas_call(functools.partial(kernel, axis), out_shape=pltpu.VMEM((mat...  117 us
    unnamed x1, local copies, waits for them, and re-layouts  2.53 us

profile of v3, /device:TPU:112, one launch (start us, length us, event | category | flops | bytes accessed | tf_op | source)
XLA Modules:
  0.0 119.7 jit_solution(3907833603347227005)
XLA Ops:
  0.0 117.2 %sums.1 = bf16[4,512,1408]{2,1,0:T(8,128)(2,1)S(1)} custom-call(bf16[4,8192,512]{2,1,0:T(8,128)(2,1)} %bitcast.2, bf16[4,8192,1408]{2,1,0:T(8,128)(2,1)} %bitcast.1.g_hbm), custom_call_target="tpu_custom_call" | custom-call | flops 47244640256 | bytes 125829120 | tf_op jit(solution)/shard_map/sums/pallas_call | solution.py:251
  117.2 2.5 %copy.4 = bf16[4,512,1408]{2,1,0:T(8,128)(2,1)} copy(bf16[4,512,1408]{2,1,0:T(8,128)(2,1)S(1)} %sums.1) | data formatting | bytes 11534336

commit v4 on v3

--- a/solution.py
+++ b/solution.py
@@ -10,6 +10,7 @@
 WIDE = 2 * TILE
 SLOTS = 4
 PIECES = 4
+OPENING = 8
 RIGHT, LEFT = 0, 1
 GROUP = 4
 HOPS = 2 * (GROUP - 1)
@@ -28,20 +29,20 @@
     ((1, 4), (2, 3)),
     ((0, 5), (4, 2), (5, 1)),
     ((0, 6), (2, 4)),
-    ((1, 5), (3, 3)),
-    ((1, 6), (5, 2)),
+    ((1, 5), (3, 3), (5, 2)),
+    ((1, 6),),
     ((0, 7), (2, 5), (3, 4)),
-    ((2, 6), (4, 3)),
-    ((1, 7), (3, 5)),
-    ((0, 8), (3, 6)),
-    ((2, 7), (4, 4)),
-    ((0, 9), (1, 8), (4, 5)),
-    ((3, 7), (4, 6)),
-    ((0, 10), (1, 9)),
+    ((4, 3),),
+    ((1, 7), (2, 6)),
+    ((0, 8), (3, 5), (4, 4)),
+    ((2, 7), (5, 3), (3, 6)),
+    ((0, 9), (1, 8)),
+    ((3, 7), (4, 5)),
+    ((0, 10), (4, 6)),
 )
 LATE = (
-    (2, 8), (1, 10), (2, 9), (3, 8), (2, 10), (3, 9), (4, 7), (3, 10),
-    (4, 8), (4, 9), (4, 10), (5, 3), (5, 4), (5, 5), (5, 6), (5, 7),
+    (1, 9), (2, 8), (1, 10), (4, 7), (2, 9), (3, 8), (2, 10), (5, 4),
+    (3, 9), (4, 8), (3, 10), (5, 5), (4, 9), (5, 6), (4, 10), (5, 7),
     (5, 8), (5, 9), (5, 10),
 )
 
@@ -94,7 +95,7 @@
         return pltpu.make_async_copy(a_hbm.at[m], a_buf.at[m % 2], a_sem.at[m % 2])
 
     def piece_copies(p):
-        step = tokens // PIECES
+        step = tokens // OPENING
         rows_p = pl.ds(p * step, step)
         m, column, _ = block_place(0)
         return (
@@ -146,24 +147,26 @@
 
     def send(n, u):
         for side in (RIGHT, LEFT):
+            if n > 0:
+                arrival(side, n - 1, u).wait_recv()
+        for side in (RIGHT, LEFT):
             k = whose(side, n)
             if n == 0:
                 first[side, u] = term_of(u, k, side).astype(first.dtype)
-            else:
-                arrival(side, n - 1, u).wait_recv()
-                if n < GROUP:
-                    total = (landed[n - 1, side, u].astype(jnp.float32) + term_of(u, k, side)).astype(first.dtype)
-                    if n < GROUP - 1:
-                        landed[n - 1, side, u] = total
-                    else:
-                        m, column = tile_place(u, me)
-                        out[m, half_rows(side), pl.ds(column, TILE)] = total
+            elif n < GROUP:
+                total = (landed[n - 1, side, u].astype(jnp.float32) + term_of(u, k, side)).astype(first.dtype)
+                if n < GROUP - 1:
+                    landed[n - 1, side, u] = total
+                else:
+                    m, column = tile_place(u, me)
+                    out[m, half_rows(side), pl.ds(column, TILE)] = total
+        for side in (RIGHT, LEFT):
             hop(side, n, u).start()
 
     def product(a, g):
         return lax.dot_general(a, g, (((0,), (0,)), ((), ())), preferred_element_type=jnp.float32)
 
-    for p in range(PIECES):
+    for p in range(OPENING):
         for copy in piece_copies(p):
             copy.start()
     for i in range(1, SLOTS):
@@ -174,9 +177,9 @@
     for side in (RIGHT, LEFT):
         pl.semaphore_signal(barrier, inc=1, device_id={axis: peer[side]}, device_id_type=pl.DeviceIdType.MESH)
 
-    step = tokens // PIECES
+    step = tokens // OPENING
     term = None
-    for p in range(PIECES):
+    for p in range(OPENING):
         for copy in piece_copies(p):
             copy.wait()
         part = product(a_buf[0, pl.ds(p * step, step)], g_buf[0, pl.ds(p * step, step)])
@@ -260,9 +263,9 @@
                 pltpu.VMEM((2, units, half, TILE), a.dtype),
                 pltpu.VMEM((GROUP - 1, 2, units, half, TILE), a.dtype),
                 pltpu.SemaphoreType.DMA((2,)),
-                pltpu.SemaphoreType.DMA((PIECES,)),
+                pltpu.SemaphoreType.DMA((OPENING,)),
                 pltpu.SemaphoreType.DMA((SLOTS,)),
-                pltpu.SemaphoreType.DMA((PIECES,)),
+                pltpu.SemaphoreType.DMA((OPENING,)),
                 pltpu.SemaphoreType.DMA((2, HOPS, units)),
                 pltpu.SemaphoreType.DMA((2, HOPS, units)),
             ],

time: 120 us -> 118 us (0.983)
  Pallas kernels: 117 us -> 115 us
    pallas_call x1, Pallas kernels: 117 us -> 115 us  [sums(): pl.pallas_call(functools.partial(kernel, axis), out_shape=pltpu.VMEM((mat...]
where the time goes in v4:
time: 118 us
  Pallas kernels  115 us (97%)
  local copies, waits for them, and re-layouts  2.53 us (2%)
    pallas_call x1, Pallas kernels, sums(): pl.pallas_call(functools.partial(kernel, axis), out_shape=pltpu.VMEM((mat...  115 us
    unnamed x1, local copies, waits for them, and re-layouts  2.53 us

profile of v4, /device:TPU:112, one launch (start us, length us, event | category | flops | bytes accessed | tf_op | source)
XLA Modules:
  0.0 117.9 jit_solution(227993963753573983)
XLA Ops:
  0.0 115.4 %sums.1 = bf16[4,512,1408]{2,1,0:T(8,128)(2,1)S(1)} custom-call(bf16[4,8192,512]{2,1,0:T(8,128)(2,1)} %bitcast.2, bf16[4,8192,1408]{2,1,0:T(8,128)(2,1)} %bitcast.1.g_hbm), custom_call_target="tpu_custom_call" | custom-call | flops 47244640256 | bytes 125829120 | tf_op jit(solution)/shard_map/sums/pallas_call | solution.py:254
  115.4 2.5 %copy.4 = bf16[4,512,1408]{2,1,0:T(8,128)(2,1)} copy(bf16[4,512,1408]{2,1,0:T(8,128)(2,1)S(1)} %sums.1) | data formatting | bytes 11534336

commit v5 on v4

--- a/solution.py
+++ b/solution.py
@@ -204,7 +204,16 @@
             a_load(3).wait()
 
         g_wait(i)
-        terms[kept] = product(a_buf[m % 2], g_buf[i % SLOTS])
+        q = i % cycle
+        narrow = q // (pairs + 1) - q // (pairs + 2) + q // (cycle - 1)
+
+        @pl.when(narrow == 0)
+        def _():
+            terms[kept] = product(a_buf[m % 2], g_buf[i % SLOTS])
+
+        @pl.when(narrow == 1)
+        def _():
+            terms[kept, :, TILE:] = product(g_buf[i % SLOTS, :, TILE:], a_buf[m % 2]).T
 
         @pl.when(i + SLOTS < blocks)
         def _():
@@ -218,12 +227,14 @@
         def _():
             a_load(3).start()
 
-        for k in range(1, blocks):
-            if SENDS[k]:
-                @pl.when(i == k)
-                def _(k=k):
-                    for n, u in SENDS[k]:
-                        send(n, u)
+        for c in range(0, blocks, 5):
+            @pl.when(i // 5 == c // 5)
+            def _(c=c):
+                for k in range(max(c, 1), min(c + 5, blocks)):
+                    @pl.when(i == k)
+                    def _(k=k):
+                        for n, u in SENDS[k]:
+                            send(n, u)
 
         return 0
 

time: 118 us -> 117 us (level)
  no operation moved by 1% of the time
where the time goes in v5:
time: 117 us
  Pallas kernels  114 us (97%)
  local copies, waits for them, and re-layouts  2.53 us (2%)
    pallas_call x1, Pallas kernels, sums(): pl.pallas_call(functools.partial(kernel, axis), out_shape=pltpu.VMEM((mat...  114 us
    unnamed x1, local copies, waits for them, and re-layouts  2.53 us

profile of v5, /device:TPU:112, one launch (start us, length us, event | category | flops | bytes accessed | tf_op | source)
XLA Modules:
  0.0 116.8 jit_solution(6555237224752421477)
XLA Ops:
  0.0 114.2 %sums.1 = bf16[4,512,1408]{2,1,0:T(8,128)(2,1)S(1)} custom-call(bf16[4,8192,512]{2,1,0:T(8,128)(2,1)} %bitcast.2, bf16[4,8192,1408]{2,1,0:T(8,128)(2,1)} %bitcast.1.g_hbm), custom_call_target="tpu_custom_call" | custom-call | flops 47244640256 | bytes 125829120 | tf_op jit(solution)/shard_map/sums/pallas_call | solution.py:265
  114.2 2.5 %copy.4 = bf16[4,512,1408]{2,1,0:T(8,128)(2,1)} copy(bf16[4,512,1408]{2,1,0:T(8,128)(2,1)S(1)} %sums.1) | data formatting | bytes 11534336
